TPU v7x, 32 devices: a whole 2x2x4 slice. The times are simulated.
32 devices in a mesh: dp: 16 (over z, y, core), mlp: 2 (over x).
Axes of the slice: x: 2, y: 2, z: 4, core: 2. Of those that a mesh axis runs over, the one named last changes fastest.
Arguments:
- block_input: bfloat16 [16, 2, 160, 1024], P('dp', 'mlp'), may hold values from -6 to 6
- span_offset: int32 [16, 2], replicated, may hold values from 0 to 15, as said below
- ln_gain: float32 [1024], replicated, may hold values from 0.5 to 1.5
- ln_bias: float32 [1024], replicated, may hold values from -3 to 3
- w_qkv: bfloat16 [1024, 3072], replicated, may hold values from -0.25 to 0.25
- b_qkv: float32 [3072], replicated, may hold values from -3 to 3
- w_out: bfloat16 [1024, 1024], replicated, may hold values from -1 to 1
- b_out: float32 [1024], replicated, may hold values from -3 to 3
- w_up: bfloat16 [1024, 4096], P(None, 'mlp'), may hold values from -0.1875 to 0.1875
- b_up: float32 [4096], P('mlp'), may hold values from -3 to 3
- w_down: bfloat16 [4096, 1024], P('mlp'), may hold values from -0.09375 to 0.09375
- b_down: float32 [1024], replicated, may hold values from -3 to 3
- cotangent: bfloat16 [16, 2, 160, 1024], P('dp', 'mlp'), may hold values from -6 to 6
Outputs:
- output: bfloat16 [16, 2, 160, 1024], P('dp', 'mlp')
- grad_input: float32 [16, 2, 160, 1024], P('dp', 'mlp')
- grad_ln_gain: float32 [1024], P('mlp')
- grad_ln_bias: float32 [1024], P('mlp')
- grad_w_qkv: float32 [1024, 3072], P(None, 'mlp')
- grad_b_qkv: float32 [3072], P('mlp')
- grad_w_out: float32 [1024, 1024], P(None, 'mlp')
- grad_b_out: float32 [1024], P('mlp')
- grad_w_up: float32 [1024, 4096], P(None, 'mlp')
- grad_b_up: float32 [4096], P('mlp')
- grad_w_down: float32 [4096, 1024], P('mlp')
- grad_b_down: float32 [1024], P('mlp')
Inputs may be any that keep to these rules, and one draw needn't show every extreme that they name: For every sequence s, span_offset[:, s] is a permutation of 0 to 15.
All inputs are finite; a program needn't handle non-finite values.
Results may differ from a plain program's by a relative error of at most 0.02.
Values may be sent and summed in bfloat16 or wider, within the bound.
A program may use at most 256 MiB of HBM per device.

v0:
```python
import math
import jax
import jax.numpy as jnp
from jax import lax
from jax.sharding import PartitionSpec as P

HEADS = 16
HEAD_DIM = 64
ROT = 16
EPSILON = 1e-05
ROPE_BASE = 10000.0
SQRT_HALF = 1.0 / math.sqrt(2.0)
INV_ROOT_TWO_PI = 1.0 / math.sqrt(2.0 * math.pi)


def rotate(values, positions, sign_factor):
    half_rot = ROT // 2
    frequency = ROPE_BASE ** (-(jnp.arange(half_rot, dtype=jnp.float32) * 2.0 / ROT))
    angles = positions.astype(jnp.float32)[:, None] * frequency[None, :]
    cosine = jnp.cos(angles)[:, None, :]
    sine_part = sign_factor * jnp.sin(angles)[:, None, :]
    first_half = values[..., :half_rot]
    second_half = values[..., half_rot:ROT]
    return jnp.concatenate(
        [
            first_half * cosine - second_half * sine_part,
            second_half * cosine + first_half * sine_part,
            values[..., ROT:],
        ],
        axis=-1,
    )


def gelu_exact(values):
    return 0.5 * values * (1.0 + lax.erf(values * SQRT_HALF))


def gelu_slope(values):
    return (
        0.5 * (1.0 + lax.erf(values * SQRT_HALF))
        + values * jnp.exp(-0.5 * values * values) * INV_ROOT_TWO_PI
    )


def piece_count(total_rows):
    count_blocks = max(1, total_rows // 1024)
    while total_rows % count_blocks:
        count_blocks += 1
    return count_blocks


def row_positions(offsets, count_rows, tok_count):
    index_all = jnp.arange(count_rows, dtype=jnp.int32)
    span_of = index_all // tok_count
    within = index_all - span_of * tok_count
    matches = span_of[:, None] == jnp.arange(offsets.shape[0], dtype=jnp.int32)[None, :]
    offset_of = jnp.sum(jnp.where(matches, offsets[None, :], 0), axis=1)
    return offset_of * tok_count + within


def contract_rows(left_mat, right_mat):
    return lax.dot_general(
        left_mat, right_mat, (((0,), (0,)), ((), ())), preferred_element_type=jnp.float32
    )


def contract_cols(left_mat, right_mat):
    return lax.dot_general(
        left_mat, right_mat, (((1,), (1,)), ((), ())), preferred_element_type=jnp.float32
    )


def local(
    block_input,
    span_offset,
    ln_gain,
    ln_bias,
    w_qkv,
    b_qkv,
    w_out,
    b_out,
    w_up,
    b_up,
    w_down,
    b_down,
    cotangent,
):
    tok_count = block_input.shape[2]
    model_width = block_input.shape[3]
    scale_dot = 1.0 / math.sqrt(HEAD_DIM)
    span_here = lax.axis_index("dp")
    seq_here = lax.axis_index("mlp")
    offsets = lax.dynamic_index_in_dim(span_offset, seq_here, axis=1, keepdims=False)
    offset_here = lax.dynamic_index_in_dim(offsets, span_here, axis=0, keepdims=False)
    positions = offset_here * tok_count + jnp.arange(tok_count, dtype=jnp.int32)
    row_data = block_input[0, 0].astype(jnp.float32)
    centre = jnp.mean(row_data, axis=-1, keepdims=True)
    centred = row_data - centre
    spread = jnp.mean(centred * centred, axis=-1, keepdims=True)
    inv_scale = lax.rsqrt(spread + EPSILON)
    unit_rows = centred * inv_scale
    normed = (unit_rows * ln_gain + ln_bias).astype(jnp.bfloat16)
    project = jnp.dot(normed, w_qkv, preferred_element_type=jnp.float32) + b_qkv
    queries = rotate(
        project[:, :model_width].reshape(tok_count, HEADS, HEAD_DIM), positions, 1.0
    ).astype(jnp.bfloat16)
    keys_here = rotate(
        project[:, model_width : 2 * model_width].reshape(tok_count, HEADS, HEAD_DIM),
        positions,
        1.0,
    ).astype(jnp.bfloat16)
    values_here = (
        project[:, 2 * model_width :].reshape(tok_count, HEADS, HEAD_DIM).astype(jnp.bfloat16)
    )
    keys_flat = keys_here.reshape(tok_count, model_width)
    values_flat = values_here.reshape(tok_count, model_width)
    start_state = (
        jnp.zeros((tok_count, HEADS, HEAD_DIM), jnp.float32),
        jnp.zeros((HEADS, tok_count), jnp.float32),
    )
    keys_piece = lax.all_gather(keys_flat, "dp", axis=0, tiled=True)
    values_piece = lax.all_gather(values_flat, "dp", axis=0, tiled=True)
    piece_rows = keys_piece.shape[0]
    blocks = piece_count(piece_rows)
    sub_rows = piece_rows // blocks
    key_pos = row_positions(offsets, piece_rows, tok_count)

    def attend_one_block(state_now, packed):
        keys_blk, values_blk, pos_blk = packed
        key_heads = keys_blk.reshape(sub_rows, HEADS, HEAD_DIM)
        value_heads = values_blk.reshape(sub_rows, HEADS, HEAD_DIM)
        scores = (
            jnp.einsum("qhd,khd->hqk", queries, key_heads, preferred_element_type=jnp.float32)
            * scale_dot
        )
        allowed = pos_blk[None, :] <= positions[:, None]
        weights_exp = jnp.where(allowed[None], jnp.exp(scores), 0.0)
        mixed_sum, totals = state_now
        mixed_sum = mixed_sum + jnp.einsum(
            "hqk,khd->qhd",
            weights_exp.astype(jnp.bfloat16),
            value_heads,
            preferred_element_type=jnp.float32,
        )
        return ((mixed_sum, totals + jnp.sum(weights_exp, axis=-1)), None)

    state_now, _unused = lax.scan(
        attend_one_block,
        start_state,
        (
            keys_piece.reshape(blocks, sub_rows, model_width),
            values_piece.reshape(blocks, sub_rows, model_width),
            key_pos.reshape(blocks, sub_rows),
        ),
    )
    mixed_sum, totals = state_now
    attended = mixed_sum / totals.T[:, :, None]
    attended_low = attended.reshape(tok_count, model_width).astype(jnp.bfloat16)
    attn_branch = jnp.dot(attended_low, w_out, preferred_element_type=jnp.float32) + b_out
    normed_all = lax.all_gather(normed, "mlp", axis=0, tiled=True)
    up_proj = jnp.dot(normed_all, w_up, preferred_element_type=jnp.float32) + b_up
    activated = gelu_exact(up_proj).astype(jnp.bfloat16)
    mlp_branch = (
        lax.psum_scatter(
            jnp.dot(activated, w_down, preferred_element_type=jnp.float32).astype(jnp.bfloat16),
            "mlp",
            scatter_dimension=0,
            tiled=True,
        ).astype(jnp.float32)
        + b_down
    )
    output = (row_data + attn_branch + mlp_branch).astype(jnp.bfloat16)
    grad_out = cotangent[0, 0]
    grad_w_out = contract_rows(attended_low, grad_out)
    grad_bias_out = jnp.sum(grad_out.astype(jnp.float32), axis=0)
    grad_all = lax.all_gather(grad_out, "mlp", axis=0, tiled=True)
    grad_w_down = contract_rows(activated, grad_all)
    grad_act = contract_cols(grad_all, w_down)
    grad_up = (grad_act * gelu_slope(up_proj)).astype(jnp.bfloat16)
    grad_w_up = contract_rows(normed_all, grad_up)
    grad_b_up = jnp.sum(grad_up.astype(jnp.float32), axis=0)
    grad_norm_mlp = lax.psum_scatter(
        contract_cols(grad_up, w_up).astype(jnp.bfloat16), "mlp", scatter_dimension=0, tiled=True
    ).astype(jnp.float32)
    grad_att = contract_cols(grad_out, w_out).reshape(tok_count, HEADS, HEAD_DIM)
    grad_mixed = (grad_att / totals.T[:, :, None]).astype(jnp.bfloat16)
    grad_totals = ((-jnp.sum(grad_att * attended, axis=-1)).T / totals).astype(jnp.bfloat16)
    grad_totals_wide = grad_totals.astype(jnp.float32)[:, :, None]
    zero_heads = jnp.zeros((tok_count, HEADS, HEAD_DIM), jnp.float32)
    grad_query_sum = zero_heads
    keys_piece = lax.all_gather(keys_flat, "dp", axis=0, tiled=True)
    values_piece = lax.all_gather(values_flat, "dp", axis=0, tiled=True)
    piece_rows = keys_piece.shape[0]
    blocks = piece_count(piece_rows)
    back_sub_rows = piece_rows // blocks
    key_pos = row_positions(offsets, piece_rows, tok_count)

    def back_one_block(running_sum, packed):
        keys_blk, values_blk, pos_blk = packed
        key_heads = keys_blk.reshape(back_sub_rows, HEADS, HEAD_DIM)
        value_heads = values_blk.reshape(back_sub_rows, HEADS, HEAD_DIM)
        scores = (
            jnp.einsum("qhd,khd->hqk", queries, key_heads, preferred_element_type=jnp.float32)
            * scale_dot
        )
        allowed = pos_blk[None, :] <= positions[:, None]
        weights_exp = jnp.where(allowed[None], jnp.exp(scores), 0.0)
        grad_exp = jnp.einsum(
            "qhd,khd->hqk", grad_mixed, value_heads, preferred_element_type=jnp.float32
        )
        grad_scores = (weights_exp * (grad_exp + grad_totals_wide)).astype(jnp.bfloat16)
        running_sum = running_sum + scale_dot * jnp.einsum(
            "hqk,khd->qhd", grad_scores, key_heads, preferred_element_type=jnp.float32
        )
        grad_key_blk = scale_dot * jnp.einsum(
            "hqk,qhd->khd", grad_scores, queries, preferred_element_type=jnp.float32
        )
        grad_value_blk = jnp.einsum(
            "hqk,qhd->khd",
            weights_exp.astype(jnp.bfloat16),
            grad_mixed,
            preferred_element_type=jnp.float32,
        )
        joined = jnp.concatenate(
            [
                grad_key_blk.reshape(back_sub_rows, model_width),
                grad_value_blk.reshape(back_sub_rows, model_width),
            ],
            axis=1,
        )
        return (running_sum, joined)

    grad_query_sum, stacked = lax.scan(
        back_one_block,
        grad_query_sum,
        (
            keys_piece.reshape(blocks, back_sub_rows, model_width),
            values_piece.reshape(blocks, back_sub_rows, model_width),
            key_pos.reshape(blocks, back_sub_rows),
        ),
    )
    grad_kv_sum = stacked.reshape(piece_rows, 2 * model_width)
    grad_kv = lax.psum_scatter(
        grad_kv_sum.astype(jnp.bfloat16), "dp", scatter_dimension=0, tiled=True
    ).astype(jnp.float32)
    grad_keys = grad_kv[:, :model_width].reshape(tok_count, HEADS, HEAD_DIM)
    grad_values = grad_kv[:, model_width:].reshape(tok_count, HEADS, HEAD_DIM)
    grad_query_pre = rotate(grad_query_sum, positions, -1.0).reshape(tok_count, model_width)
    grad_key_pre = rotate(grad_keys, positions, -1.0).reshape(tok_count, model_width)
    grad_project = jnp.concatenate(
        [grad_query_pre, grad_key_pre, grad_values.reshape(tok_count, model_width)], axis=1
    ).astype(jnp.bfloat16)
    grad_w_qkv = contract_rows(normed, grad_project)
    grad_b_qkv = jnp.sum(grad_project.astype(jnp.float32), axis=0)
    grad_normed = contract_cols(grad_project, w_qkv) + grad_norm_mlp
    grad_ln_gain = jnp.sum(grad_normed * unit_rows, axis=0)
    grad_ln_bias = jnp.sum(grad_normed, axis=0)
    grad_unit = grad_normed * ln_gain
    grad_rows = inv_scale * (
        grad_unit
        - jnp.mean(grad_unit, axis=-1, keepdims=True)
        - unit_rows * jnp.mean(grad_unit * unit_rows, axis=-1, keepdims=True)
    )
    grad_input = (grad_out.astype(jnp.float32) + grad_rows).reshape(1, 1, tok_count, model_width)
    part_qkv, part_out, part_bqkv, part_bias, part_gain, part_shift = (
        lax.psum_scatter(
            grad_w_qkv.astype(jnp.bfloat16), "mlp", scatter_dimension=1, tiled=True
        ).astype(jnp.float32),
        lax.psum_scatter(
            grad_w_out.astype(jnp.bfloat16), "mlp", scatter_dimension=1, tiled=True
        ).astype(jnp.float32),
        lax.psum_scatter(
            grad_b_qkv.astype(jnp.bfloat16), "mlp", scatter_dimension=0, tiled=True
        ).astype(jnp.float32),
        lax.psum_scatter(
            grad_bias_out.astype(jnp.bfloat16), "mlp", scatter_dimension=0, tiled=True
        ).astype(jnp.float32),
        lax.psum_scatter(
            grad_ln_gain.astype(jnp.bfloat16), "mlp", scatter_dimension=0, tiled=True
        ).astype(jnp.float32),
        lax.psum_scatter(
            grad_ln_bias.astype(jnp.bfloat16), "mlp", scatter_dimension=0, tiled=True
        ).astype(jnp.float32),
    )
    summed = (
        lax.psum(part_qkv.astype(jnp.bfloat16), "dp").astype(jnp.float32),
        lax.psum(part_out.astype(jnp.bfloat16), "dp").astype(jnp.float32),
        lax.psum(part_bqkv.astype(jnp.bfloat16), "dp").astype(jnp.float32),
        lax.psum(part_bias.astype(jnp.bfloat16), "dp").astype(jnp.float32),
        lax.psum(part_gain.astype(jnp.bfloat16), "dp").astype(jnp.float32),
        lax.psum(part_shift.astype(jnp.bfloat16), "dp").astype(jnp.float32),
        lax.psum(grad_w_up.astype(jnp.bfloat16), "dp").astype(jnp.float32),
        lax.psum(grad_b_up.astype(jnp.bfloat16), "dp").astype(jnp.float32),
        lax.psum(grad_w_down.astype(jnp.bfloat16), "dp").astype(jnp.float32),
    )
    return (
        output.reshape(1, 1, tok_count, model_width),
        grad_input,
        summed[4],
        summed[5],
        summed[0],
        summed[2],
        summed[1],
        summed[3],
        summed[6],
        summed[7],
        summed[8],
        summed[3],
    )


def solution(mesh):
    return jax.shard_map(
        local,
        mesh=mesh,
        in_specs=(
            P("dp", "mlp", None, None),
            P(),
            P(),
            P(),
            P(),
            P(),
            P(),
            P(),
            P(None, "mlp"),
            P("mlp"),
            P("mlp", None),
            P(),
            P("dp", "mlp", None, None),
        ),
        out_specs=(
            P("dp", "mlp", None, None),
            P("dp", "mlp", None, None),
            P("mlp"),
            P("mlp"),
            P(None, "mlp"),
            P("mlp"),
            P(None, "mlp"),
            P("mlp"),
            P(None, "mlp"),
            P("mlp"),
            P("mlp", None),
            P("mlp"),
        ),
        check_vma=False,
    )
```

profile of v0, /device:TPU:0, one launch (start us, length us, event | category | flops | bytes accessed | tf_op | source)
XLA Modules:
  0.0 848.6 jit_solution(7495591158141131622)
XLA Ops:
  38.3 52.1 %all-gather.6.cloned.1.call-done = bf16[2560,1024]{1,0:T(8,128)(2,1)} async-done(((bf16[160,1024]{1,0:T(8,128)(2,1)}), bf16[2560,1024]{1,0:T(8,128)(2,1)}) %all-gather.6.cloned.1.call-update) | async-done | bytes 5242896 | tf_op jit(solution)/shard_map/all_gather | solution.py:121
  90.4 7.9 copy.85
  98.3 49.4 %all-gather.4.cloned.1.call-done = bf16[2560,1024]{1,0:T(8,128)(2,1)} async-done(((bf16[160,1024]{1,0:T(8,128)(2,1)}), bf16[2560,1024]{1,0:T(8,128)(2,1)}) %all-gather.4.cloned.1.call-update) | async-done | bytes 5242896 | tf_op jit(solution)/shard_map/all_gather | solution.py:122
  147.7 7.9 copy.84
  155.5 40.2 %while.26 = (s32[]{:T(128)}, f32[160,16,64]{0,2,1:T(8,128)}, f32[16,160]{1,0:T(8,128)S(1)}, bf16[2,1280,1024]{1,2,0:T(8,128)(2,1)}, s32[2,1280]{1,0:T(2,128)S(1)...) while((s32[]{:T(128)}, f32[160,16,64]{0,2,1:T(8,128)}, ...), condition=%wide.region_5.6_spmd.clone, body=%wide.region_3.5_spmd.clone.sunk | while | flops 859056768 | bytes 44253560 | solution.py:147
  166.7 8.9 %fusion.125 = f32[160,16,64]{0,2,1:T(8,128)} fusion(bf16[1280,16,64]{0,2,1:T(8,128)(2,1)} %bitcast.209, f32[16,1280,160]{1,2,0:T(8,128)} %get-tuple-element.480, pred[160,1280]{1,0:T(8,128)(4,1)S(1)} %broadcast_compare_fusion.4, f32[160,16,64]{0,2,1:T(8,128)} %get-tuple-element.505, pred[]{:T(512)S(6)} %compare.6), kind=kOutput, calls=%fused_computation.10.clone.1 | convolution fusion | flops 429588480 | bytes 17244160 | tf_op jit(solution)/shard_map/while/body/eval_jaxpr/hqk,khd->qhd/dot_general | solution.py:139
  186.7 9.1 %fusion.125 = f32[160,16,64]{0,2,1:T(8,128)} fusion(bf16[1280,16,64]{0,2,1:T(8,128)(2,1)} %bitcast.209, f32[16,1280,160]{1,2,0:T(8,128)} %get-tuple-element.480, pred[160,1280]{1,0:T(8,128)(4,1)S(1)} %broadcast_compare_fusion.4, f32[160,16,64]{0,2,1:T(8,128)} %get-tuple-element.505, pred[]{:T(512)S(6)} %compare.6), kind=kOutput, calls=%fused_computation.10.clone.1 | convolution fusion | flops 429588480 | bytes 17244160 | tf_op jit(solution)/shard_map/while/body/eval_jaxpr/hqk,khd->qhd/dot_general | solution.py:139
  198.7 110.8 %while.27 = (s32[]{:T(128)}, f32[160,16,64]{0,2,1:T(8,128)}, bf16[2,1280,2048]{2,1,0:T(8,128)(2,1)}, bf16[2,1280,1024]{1,2,0:T(8,128)(2,1)}, s32[2,1280]{1,0:T(2...) while((s32[]{:T(128)}, f32[160,16,64]{0,2,1:T(8,128)}, ...), condition=%wide.region_9.10_spmd.clone, body=%wide.region_8.9_spmd.clone.sunk | while | flops 2137170048 | bytes 206425072 | solution.py:233
  210.1 9.9 %fusion.137 = bf16[16,160,1280]{2,1,0:T(8,128)(2,1)S(1)} fusion(f32[16,1280,160]{1,2,0:T(8,128)} %fusion.136, bf16[1280,16,64]{0,2,1:T(8,128)(2,1)} %bitcast.211, bf16[160,16,64]{0,2,1:T(8,128)(2,1)} %get-tuple-element.555, f32[16,160]{1,0:T(8,128)S(1)} %bitcast.219, pred[160,1280]{1,0:T(8,128)(4,1)S(1)} %broadcast_compare_fusion.5), kind=kOutput, calls=%fused_computation.20.clone.1 | convolution fusion | flops 435814400 | bytes 22824960 | tf_op jit(solution)/shard_map/while/body/eval_jaxpr/qhd,khd->hqk/dot_general | solution.py:208
  233.6 8.0 copy.108
  247.1 6.9 fusion.138
  265.2 9.9 %fusion.137 = bf16[16,160,1280]{2,1,0:T(8,128)(2,1)S(1)} fusion(f32[16,1280,160]{1,2,0:T(8,128)} %fusion.136, bf16[1280,16,64]{0,2,1:T(8,128)(2,1)} %bitcast.211, bf16[160,16,64]{0,2,1:T(8,128)(2,1)} %get-tuple-element.555, f32[16,160]{1,0:T(8,128)S(1)} %bitcast.219, pred[160,1280]{1,0:T(8,128)(4,1)S(1)} %broadcast_compare_fusion.5), kind=kOutput, calls=%fused_computation.20.clone.1 | convolution fusion | flops 435814400 | bytes 22824960 | tf_op jit(solution)/shard_map/while/body/eval_jaxpr/qhd,khd->hqk/dot_general | solution.py:208
  288.7 8.0 copy.108
  302.4 7.1 fusion.138
  326.5 101.3 %reduce-scatter.8.cloned.1.call-done = bf16[160,2048]{1,0:T(8,128)(2,1)} async-done(((bf16[2560,2048]{1,0:T(8,128)(2,1)}), bf16[160,2048]{1,0:T(8,128)(2,1)}) %reduce-scatter.8.cloned.1.call-update) | async-done | bytes 655376 | tf_op jit(solution)/shard_map/reduce_scatter | solution.py:243
  442.0 17.8 %all_gather.16 = bf16[320,1024]{1,0:T(8,128)(2,1)S(1)} all-gather(bf16[160,1024]{1,0:T(8,128)(2,1)S(1)} %copy-done.8), channel_id=1, replica_groups=mesh['dp'=16,'mlp'=2] {'mlp'}, dimensions={0}, use_global_device_ids=true | all-gather | bytes 983040 | tf_op jit(solution)/shard_map/all_gather | solution.py:160
  469.1 9.4 %all-gather = bf16[1,1,320,1024]{3,2,1,0:T(8,128)(2,1)S(1)} all-gather(bf16[1,1,160,1024]{3,2,1,0:T(8,128)(2,1)S(1)} %copy-done.11), channel_id=2, replica_groups=mesh['dp'=16,'mlp'=2] {'mlp'}, dimensions={2}, use_global_device_ids=true | all-gather | bytes 983040 | tf_op jit(solution)/shard_map/all_gather | solution.py:176
  499.1 49.8 %reduce-scatter.12.cloned.1.call-done = bf16[1024,1536]{1,0:T(8,128)(2,1)} async-done(((bf16[1024,3072]{1,0:T(8,128)(2,1)}), bf16[1024,1536]{1,0:T(8,128)(2,1)}) %reduce-scatter.12.cloned.1.call-update) | async-done | bytes 3145744 | tf_op jit(solution)/shard_map/reduce_scatter | solution.py:266
  551.5 16.2 %reduce-scatter.6.cloned.1.call-done = bf16[160,1024]{1,0:T(8,128)(2,1)} async-done(((bf16[320,1024]{1,0:T(8,128)(2,1)}), bf16[160,1024]{1,0:T(8,128)(2,1)}) %reduce-scatter.6.cloned.1.call-update) | async-done | bytes 327696 | tf_op jit(solution)/shard_map/reduce_scatter | solution.py:164
  570.4 15.7 %reduce-scatter.10.cloned.1.call-done = bf16[160,1024]{1,0:T(8,128)(2,1)} async-done(((bf16[320,1024]{1,0:T(8,128)(2,1)}), bf16[160,1024]{1,0:T(8,128)(2,1)}) %reduce-scatter.10.cloned.1.call-update) | async-done | bytes 327696 | tf_op jit(solution)/shard_map/reduce_scatter | solution.py:182
  592.2 6.9 all-reduce.6
  599.4 63.3 %all-reduce.4 = (bf16[512]{0:T(512)(128)(2,1)S(1)}, bf16[512]{0:T(512)(128)(2,1)S(1)}, bf16[1536]{0:T(1024)(128)(2,1)S(1)}, bf16[512]{0:T(512)(128)(2,1)S(1)}, bf16[2048]{0:T(1024)(128)(2,1)S(1)}) all-reduce(bf16[512]{0:T(512)(128)(2,1)S(1)} %dynamic-slice.2, ...), channel_id=1, replica_groups=mesh['dp'=16,'mlp'=2] {'dp'}, use_global_device_ids=true, to_apply=%region_16.17 | all-reduce | flops 5120 | bytes 20480 | tf_op jit(solution)/shard_map/psum | solution.py:290
  667.2 157.0 %all-reduce.9.cloned.1.call-done = (bf16[1024,1536]{1,0:T(8,128)(2,1)}, bf16[1024,512]{1,0:T(8,128)(2,1)}, bf16[1024,2048]{1,0:T(8,128)(2,1)}, bf16[2048,1024]{1,0:T(8,128)(2,1)}) async-done(((bf16[1024,1536]{1,0:T(8,128)(2,1)}, bf16[1024,512]{1,0:T(8,128)(2,1)}, bf16[1024,2048]{1,0:T(8,128)(2,1)}, bf16[2048,1024]{1,0:T(8,128)(2,1)}), (bf16[1024,1536]{1,0:T(8,128)(2,1)}, bf16[1024,512]{1,0:T(8,128)(2,1)}, ...) | async-done | bytes 12582928 | tf_op jit(solution)/shard_map/psum | solution.py:286
  824.2 6.8 convert_element_type.175
  (211 shorter events, 202.0 us)
Async XLA Ops:
  7.2 188.6 %copy-start = (bf16[1024,1024]{1,0:T(8,128)(2,1)S(1)}, bf16[1024,1024]{1,0:T(8,128)(2,1)}, u32[]{:S(2)}) copy-start(bf16[1024,1024]{1,0:T(8,128)(2,1)} %param.23) | copy-start | bytes 6291460
  7.2 83.2 %all-gather.6.cloned.1.call-start = ((), (), s32[]{:S(2)}) async-start(), calls=%async_computation.6 | async-start | bytes 5570560 | tf_op jit(solution)/shard_map/all_gather | solution.py:121
  10.2 15.1 %copy-start.17 = (f32[160,8]{1,0:T(8,128)}, f32[160,8]{1,0:T(8,128)S(1)}, u32[]{:S(2)}) copy-start(f32[160,8]{1,0:T(8,128)S(1)} %copy.82) | copy-start | bytes 15364
  31.8 115.8 %all-gather.4.cloned.1.call-start = ((), (), s32[]{:S(2)}) async-start(), calls=%async_computation.5 | async-start | bytes 5570560 | tf_op jit(solution)/shard_map/all_gather | solution.py:122
  33.8 394.0 %reduce-scatter.8.cloned.1.call-start = ((), (), s32[]{:S(2)}) async-start(), calls=%async_computation.8 | async-start | bytes 11141120 | tf_op jit(solution)/shard_map/reduce_scatter | solution.py:243
  155.5 40.2 %copy-start.10 = (bf16[1,1,160,1024]{3,2,1,0:T(8,128)(2,1)S(1)}, bf16[1,1,160,1024]{3,2,1,0:T(8,128)(2,1)}, u32[]{:S(2)}) copy-start(bf16[1,1,160,1024]{3,2,1,0:T(8,128)(2,1)} %param.29) | copy-start | bytes 983044
  220.1 7.1 copy-start.2
  275.2 7.1 copy-start.2
  309.5 189.6 %reduce-scatter.14.cloned.1.call-start = ((), (), s32[]{:S(2)}) async-start(), calls=%async_computation.11 | async-start | bytes 3145728 | tf_op jit(solution)/shard_map/reduce_scatter | solution.py:269
  313.5 235.4 %reduce-scatter.12.cloned.1.call-start = ((), (), s32[]{:S(2)}) async-start(), calls=%async_computation.10 | async-start | bytes 9437184 | tf_op jit(solution)/shard_map/reduce_scatter | solution.py:266
  317.7 6.9 copy-start.16
  441.9 17.9 %copy-start.35 = (f32[2048]{0:T(1024)S(1)}, f32[2048]{0:T(1024)}, u32[]{:S(2)}) copy-start(f32[2048]{0:T(1024)} %param.26) | copy-start | bytes 24580
  441.9 125.8 %reduce-scatter.6.cloned.1.call-start = ((), (), s32[]{:S(2)}) async-start(), calls=%async_computation.7 | async-start | bytes 983040 | tf_op jit(solution)/shard_map/reduce_scatter | solution.py:164
  459.8 6.8 copy-start.33
  469.1 117.0 %reduce-scatter.10.cloned.1.call-start = ((), (), s32[]{:S(2)}) async-start(), calls=%async_computation.9 | async-start | bytes 983040 | tf_op jit(solution)/shard_map/reduce_scatter | solution.py:182
  478.5 7.5 copy-start.34
  488.5 335.7 %all-reduce.9.cloned.1.call-start = ((), (), s32[]{:S(2)}) async-start(), calls=%async_computation.12 | async-start | bytes 25165824 | tf_op jit(solution)/shard_map/psum | solution.py:286
  548.9 18.8 %copy-start.6 = (bf16[1,1,160,1024]{3,2,1,0:T(8,128)(2,1)S(1)}, bf16[1,1,160,1024]{3,2,1,0:T(8,128)(2,1)}, u32[]{:S(2)}) copy-start(bf16[1,1,160,1024]{3,2,1,0:T(8,128)(2,1)} %param.17) | copy-start | bytes 983044
  548.9 18.8 %copy-start.24 = (f32[1024]{0:T(1024)S(1)}, f32[1024]{0:T(1024)}, u32[]{:S(2)}) copy-start(f32[1024]{0:T(1024)} %param.28) | copy-start | bytes 12292
  548.9 18.8 %copy-start.25 = (f32[1024]{0:T(1024)S(1)}, f32[1024]{0:T(1024)}, u32[]{:S(2)}) copy-start(f32[1024]{0:T(1024)} %param.24) | copy-start | bytes 12292
  549.0 37.1 %copy-start.27 = (f32[160]{0:T(256)S(1)}, f32[160]{0:T(256)}, u32[]{:S(2)}) copy-start(f32[160]{0:T(256)} %copy-done.26) | copy-start | bytes 1924
  549.0 37.1 %copy-start.28 = (f32[1024]{0:T(1024)S(1)}, f32[1024]{0:T(1024)}, u32[]{:S(2)}) copy-start(f32[1024]{0:T(1024)} %param.19) | copy-start | bytes 12292
  549.0 37.1 %copy-start.30 = (f32[160]{0:T(256)S(1)}, f32[160]{0:T(256)}, u32[]{:S(2)}) copy-start(f32[160]{0:T(256)} %copy-done.29) | copy-start | bytes 1924
  663.9 176.8 %copy-start.31 = (f32[512]{0:T(512)}, f32[512]{0:T(512)S(1)}, u32[]{:S(2)}) copy-start(f32[512]{0:T(512)S(1)} %convert_element_type.173) | copy-start | bytes 6148
  (27 other events, 97.3 us)
Sparse Core Ops, SparseCore 0:
  31.9 58.4 all-gather.5
  93.3 54.3 all-gather.3
  309.6 118.0 reduce-scatter.7
  430.4 38.5 reduce-scatter.13
  471.8 77.1 reduce-scatter.11
  551.6 16.0 reduce-scatter.5
  570.0 16.0 reduce-scatter.9
  591.2 232.9 all-reduce.8
where the time goes:
time: 855 us; the launch traced here: 849 us
  waiting for transfers between devices  442 us (52%)
  matrix products  139 us (16%)
  local copies, waits for them, and re-layouts  107 us (13%)
  blocking collectives  97.4 us (11%)
  other arithmetic  44.8 us (5%)
  between operations  17 us (2%)
    psum x1, waiting for transfers between devices, local(): lax.psum(part_qkv.astype(jnp.bfloat16), 'dp').astype(jnp.float32)  157 us
    reduce_scatter x1, waiting for transfers between devices, local(): lax.psum_scatter(grad_kv_sum.astype(jnp.bfloat16), 'dp', scatter_dimensio...  101 us
    psum x1, blocking collectives, local(): lax.psum(part_gain.astype(jnp.bfloat16), 'dp').astype(jnp.float32)  63.3 us
    all_gather x1, waiting for transfers between devices, local(): keys_piece = lax.all_gather(keys_flat, 'dp', axis=0, tiled=True)  52.1 us
    reduce_scatter x1, waiting for transfers between devices, local(): lax.psum_scatter(grad_w_qkv.astype(jnp.bfloat16), 'mlp', scatter_dimensio...  49.8 us
    all_gather x1, waiting for transfers between devices, local(): values_piece = lax.all_gather(values_flat, 'dp', axis=0, tiled=True)  49.4 us
    dynamic_update_slice x4, local copies, waits for them, and re-layouts, local(): lax.scan(back_one_block, grad_query_sum, (keys_piece.reshape(blocks, back...  27.2 us
    unnamed x83, local copies, waits for them, and re-layouts  23 us
  transfers between devices with their start and end apart: 8, of which 7 were waited for; matrix products, arithmetic and copies ran while one was open for 10% of the time, Pallas kernels for 0%

commit v1 on v0

--- a/solution.py
+++ b/solution.py
@@ -11,6 +11,25 @@
 ROPE_BASE = 10000.0
 SQRT_HALF = 1.0 / math.sqrt(2.0)
 INV_ROOT_TWO_PI = 1.0 / math.sqrt(2.0 * math.pi)
+
+
+def _test_lines(x_part, pos_dim):
+    x_part = jnp.moveaxis(x_part, 0, pos_dim)
+    v1 = x_part.shape
+    return x_part.reshape(*v1[:pos_dim], v1[pos_dim] * v1[pos_dim + 1], *v1[pos_dim + 2 :])
+
+
+def end_slices_up(patch, comm_axis):
+    outer, field_out = (lax.axis_size(comm_axis), lax.axis_index(comm_axis))
+    val2, new = (patch[None], 1)
+    while new < outer:
+        built = lax.ppermute(val2, comm_axis, tuple(((ii, ii ^ new) for ii in range(outer))))
+        block_next = field_out & new == 0
+        val2 = jnp.concatenate(
+            [jnp.where(block_next, val2, built), jnp.where(block_next, built, val2)]
+        )
+        new *= 2
+    return val2
 
 
 def rotate(values, positions, sign_factor):
@@ -118,7 +137,7 @@
         jnp.zeros((tok_count, HEADS, HEAD_DIM), jnp.float32),
         jnp.zeros((HEADS, tok_count), jnp.float32),
     )
-    keys_piece = lax.all_gather(keys_flat, "dp", axis=0, tiled=True)
+    keys_piece = _test_lines(end_slices_up(keys_flat, "dp"), 0)
     values_piece = lax.all_gather(values_flat, "dp", axis=0, tiled=True)
     piece_rows = keys_piece.shape[0]
     blocks = piece_count(piece_rows)

time: 855 us -> 998 us (1.17)
  waiting for transfers between devices: 442 us -> 542 us
  matrix products: 139 us -> 155 us
  other arithmetic: 44.8 us -> 56.1 us
    ppermute x0 -> x4, waiting for transfers between devices: none -> 200 us  [end_slices_up(): lax.ppermute(val2, comm_axis, tuple(((ii, ii ^ new) for ii in range(outer...]
    all_gather x1, waiting for transfers between devices: 52.1 us -> 0.02 us  [local(): keys_piece = lax.all_gather(keys_flat, 'dp', axis=0, tiled=True)]
    all_gather x1, waiting for transfers between devices: 49.4 us -> 0.01 us  [local(): values_piece = lax.all_gather(values_flat, 'dp', axis=0, tiled=True)]
    dynamic_slice x8 -> x16, local copies, waits for them, and re-layouts: 17.6 us -> 38.8 us  [local(): lax.scan(attend_one_block, start_state, (keys_piece.reshape(blocks, sub_r...]
    unnamed x83 -> x92, local copies, waits for them, and re-layouts: 23 us -> 19.4 us
  transfers between devices with their start and end apart: 8 -> 12, of which waited for: 7 -> 9; matrix products, arithmetic and copies ran while one was open for 10% -> 17% of each run, Pallas kernels for 0% -> 0%
where the time goes in v1:
time: 998 us; the launch traced here: 991 us
  waiting for transfers between devices  542 us (54%)
  matrix products  155 us (16%)
  local copies, waits for them, and re-layouts  115 us (12%)
  blocking collectives  97.3 us (10%)
  other arithmetic  56.1 us (6%)
  between operations  16.9 us (2%)
    ppermute x4, waiting for transfers between devices, end_slices_up(): lax.ppermute(val2, comm_axis, tuple(((ii, ii ^ new) for ii in range(outer...  200 us
    psum x1, waiting for transfers between devices, local(): lax.psum(part_qkv.astype(jnp.bfloat16), 'dp').astype(jnp.float32)  157 us
    reduce_scatter x1, waiting for transfers between devices, local(): lax.psum_scatter(grad_kv_sum.astype(jnp.bfloat16), 'dp', scatter_dimensio...  103 us
    psum x1, blocking collectives, local(): lax.psum(part_gain.astype(jnp.bfloat16), 'dp').astype(jnp.float32)  63.2 us
    reduce_scatter x1, waiting for transfers between devices, local(): lax.psum_scatter(grad_w_qkv.astype(jnp.bfloat16), 'mlp', scatter_dimensio...  49.9 us
    dynamic_slice x16, local copies, waits for them, and re-layouts, local(): lax.scan(attend_one_block, start_state, (keys_piece.reshape(blocks, sub_r...  38.8 us
    dynamic_update_slice x4, local copies, waits for them, and re-layouts, local(): lax.scan(back_one_block, grad_query_sum, (keys_piece.reshape(blocks, back...  27.4 us
  transfers between devices with their start and end apart: 12, of which 9 were waited for; matrix products, arithmetic and copies ran while one was open for 17% of the time, Pallas kernels for 0%

profile of v1, /device:TPU:0, one launch (start us, length us, event | category | flops | bytes accessed | tf_op | source)
XLA Modules:
  0.0 990.8 jit_solution(10866736295139719446)
XLA Ops:
  32.9 16.0 %collective-permute-done.1 = bf16[2,160,1024]{2,1,0:T(8,128)(2,1)} collective-permute-done((bf16[2,160,1024]{2,1,0:T(8,128)(2,1)S(1)}, bf16[2,160,1024]{2,1,0:T(8,128)(2,1)}, u32[]{:S(2)}, u32[]{:S(2)}) %collective-permute-start.1) | collective-permute-done | bytes 655392 | tf_op jit(solution)/shard_map/ppermute | solution.py:26
  53.9 46.0 %collective-permute-done.2 = bf16[4,160,1024]{2,1,0:T(8,128)(2,1)} collective-permute-done((bf16[4,160,1024]{2,1,0:T(8,128)(2,1)}, bf16[4,160,1024]{2,1,0:T(8,128)(2,1)}, u32[]{:S(2)}, u32[]{:S(2)}) %collective-permute-start.2) | collective-permute-done | bytes 1310752 | tf_op jit(solution)/shard_map/ppermute | solution.py:26
  114.9 136.5 %collective-permute-done.3 = bf16[8,160,1024]{2,1,0:T(8,128)(2,1)} collective-permute-done((bf16[8,160,1024]{2,1,0:T(8,128)(2,1)}, bf16[8,160,1024]{2,1,0:T(8,128)(2,1)}, u32[]{:S(2)}, u32[]{:S(2)}) %collective-permute-start.3) | collective-permute-done | bytes 2621472 | tf_op jit(solution)/shard_map/ppermute | solution.py:26
  256.5 7.9 copy.84
  264.4 59.1 %while.26 = (s32[]{:T(128)}, f32[160,16,64]{0,2,1:T(8,128)}, f32[16,160]{1,0:T(8,128)S(1)}, bf16[2,1280,1024]{1,2,0:T(8,128)(2,1)}, s32[2,1280]{1,0:T(2,128)S(1)...) while((s32[]{:T(128)}, f32[160,16,64]{0,2,1:T(8,128)}, ...), condition=%wide.region_5.6_spmd.clone, body=%wide.region_3.5_spmd.clone.sunk | while | flops 859056768 | bytes 65225132 | solution.py:166
  273.3 10.0 %fusion.124 = (f32[16,160]{1,0:T(8,128)S(1)}, f32[16,1280,160]{1,2,0:T(8,128)}) fusion(pred[160,1280]{1,0:T(8,128)(4,1)} %broadcast_compare_fusion.4, bf16[1280,16,64]{0,2,1:T(8,128)(2,1)} %bitcast.214, bf16[160,16,64]{0,2,1:T(8,128)(2,1)} %get-tuple-element.514), kind=kOutput, calls=%fused_computation.3.clone.1 | convolution fusion | flops 429258240 | bytes 16271360 | tf_op jit(solution)/shard_map/while/body/eval_jaxpr/qhd,khd->hqk/dot_general | solution.py:152
  285.0 8.8 fusion.125
  302.7 10.0 %fusion.124 = (f32[16,160]{1,0:T(8,128)S(1)}, f32[16,1280,160]{1,2,0:T(8,128)}) fusion(pred[160,1280]{1,0:T(8,128)(4,1)} %broadcast_compare_fusion.4, bf16[1280,16,64]{0,2,1:T(8,128)(2,1)} %bitcast.214, bf16[160,16,64]{0,2,1:T(8,128)(2,1)} %get-tuple-element.514), kind=kOutput, calls=%fused_computation.3.clone.1 | convolution fusion | flops 429258240 | bytes 16271360 | tf_op jit(solution)/shard_map/while/body/eval_jaxpr/qhd,khd->hqk/dot_general | solution.py:152
  314.4 9.1 fusion.125
  326.4 124.0 %while.27 = (s32[]{:T(128)}, f32[160,16,64]{0,2,1:T(8,128)}, bf16[2,1280,2048]{2,1,0:T(8,128)(2,1)}, bf16[2,1280,1024]{2,1,0:T(8,128)(2,1)}, s32[2,1280]{1,0:T(2...) while((s32[]{:T(128)}, f32[160,16,64]{0,2,1:T(8,128)}, ...), condition=%wide.region_9.10_spmd.clone, body=%wide.region_8.9_spmd.clone.sunk | while | flops 2137170048 | bytes 172346448 | solution.py:252
  334.7 8.6 fusion.136
  345.2 10.0 %fusion.137 = bf16[16,160,1280]{2,1,0:T(8,128)(2,1)S(1)} fusion(f32[16,1280,160]{1,2,0:T(8,128)} %fusion.136, bf16[1280,16,64]{0,2,1:T(8,128)(2,1)} %bitcast.216, bf16[160,16,64]{0,2,1:T(8,128)(2,1)} %get-tuple-element.549, f32[16,160]{1,0:T(8,128)S(1)} %bitcast.225, pred[160,1280]{1,0:T(8,128)(4,1)S(1)} %broadcast_compare_fusion.5), kind=kOutput, calls=%fused_computation.20.clone.1 | convolution fusion | flops 435814400 | bytes 22824960 | tf_op jit(solution)/shard_map/while/body/eval_jaxpr/qhd,khd->hqk/dot_general | solution.py:227
  367.9 8.0 copy.114
  396.5 8.6 fusion.136
  407.1 10.0 %fusion.137 = bf16[16,160,1280]{2,1,0:T(8,128)(2,1)S(1)} fusion(f32[16,1280,160]{1,2,0:T(8,128)} %fusion.136, bf16[1280,16,64]{0,2,1:T(8,128)(2,1)} %bitcast.216, bf16[160,16,64]{0,2,1:T(8,128)(2,1)} %get-tuple-element.549, f32[16,160]{1,0:T(8,128)S(1)} %bitcast.225, pred[160,1280]{1,0:T(8,128)(4,1)S(1)} %broadcast_compare_fusion.5), kind=kOutput, calls=%fused_computation.20.clone.1 | convolution fusion | flops 435814400 | bytes 22824960 | tf_op jit(solution)/shard_map/while/body/eval_jaxpr/qhd,khd->hqk/dot_general | solution.py:227
  429.8 8.0 copy.114
  467.2 103.1 %reduce-scatter.8.cloned.1.call-done = bf16[160,2048]{1,0:T(8,128)(2,1)} async-done(((bf16[2560,2048]{1,0:T(8,128)(2,1)}), bf16[160,2048]{1,0:T(8,128)(2,1)}) %reduce-scatter.8.cloned.1.call-update) | async-done | bytes 655376 | tf_op jit(solution)/shard_map/reduce_scatter | solution.py:262
  584.5 17.8 %all_gather.14 = bf16[320,1024]{1,0:T(8,128)(2,1)S(1)} all-gather(bf16[160,1024]{1,0:T(8,128)(2,1)S(1)} %copy-done.12), channel_id=1, replica_groups=mesh['dp'=16,'mlp'=2] {'mlp'}, dimensions={0}, use_global_device_ids=true | all-gather | bytes 983040 | tf_op jit(solution)/shard_map/all_gather | solution.py:179
  611.6 9.3 all-gather
  641.5 49.9 %reduce-scatter.12.cloned.1.call-done = bf16[1024,1536]{1,0:T(8,128)(2,1)} async-done(((bf16[1024,3072]{1,0:T(8,128)(2,1)}), bf16[1024,1536]{1,0:T(8,128)(2,1)}) %reduce-scatter.12.cloned.1.call-update) | async-done | bytes 3145744 | tf_op jit(solution)/shard_map/reduce_scatter | solution.py:285
  694.0 16.2 %reduce-scatter.6.cloned.1.call-done = bf16[160,1024]{1,0:T(8,128)(2,1)} async-done(((bf16[320,1024]{1,0:T(8,128)(2,1)}), bf16[160,1024]{1,0:T(8,128)(2,1)}) %reduce-scatter.6.cloned.1.call-update) | async-done | bytes 327696 | tf_op jit(solution)/shard_map/reduce_scatter | solution.py:183
  712.9 15.7 %reduce-scatter.10.cloned.1.call-done = bf16[160,1024]{1,0:T(8,128)(2,1)} async-done(((bf16[320,1024]{1,0:T(8,128)(2,1)}), bf16[160,1024]{1,0:T(8,128)(2,1)}) %reduce-scatter.10.cloned.1.call-update) | async-done | bytes 327696 | tf_op jit(solution)/shard_map/reduce_scatter | solution.py:201
  741.9 63.2 %all-reduce.4 = (bf16[512]{0:T(512)(128)(2,1)S(1)}, bf16[512]{0:T(512)(128)(2,1)S(1)}, bf16[1536]{0:T(1024)(128)(2,1)S(1)}, bf16[512]{0:T(512)(128)(2,1)S(1)}, bf16[2048]{0:T(1024)(128)(2,1)S(1)}) all-reduce(bf16[512]{0:T(512)(128)(2,1)S(1)} %dynamic-slice.2, ...), channel_id=1, replica_groups=mesh['dp'=16,'mlp'=2] {'dp'}, use_global_device_ids=true, to_apply=%region_16.17 | all-reduce | flops 5120 | bytes 20480 | tf_op jit(solution)/shard_map/psum | solution.py:309
  809.7 157.1 %all-reduce.9.cloned.1.call-done = (bf16[1024,1536]{1,0:T(8,128)(2,1)}, bf16[1024,512]{1,0:T(8,128)(2,1)}, bf16[1024,2048]{1,0:T(8,128)(2,1)}, bf16[2048,1024]{1,0:T(8,128)(2,1)}) async-done(((bf16[1024,1536]{1,0:T(8,128)(2,1)}, bf16[1024,512]{1,0:T(8,128)(2,1)}, bf16[1024,2048]{1,0:T(8,128)(2,1)}, bf16[2048,1024]{1,0:T(8,128)(2,1)}), (bf16[1024,1536]{1,0:T(8,128)(2,1)}, bf16[1024,512]{1,0:T(8,128)(2,1)}, ...) | async-done | bytes 12582928 | tf_op jit(solution)/shard_map/psum | solution.py:305
  (274 shorter events, 243.8 us)
Async XLA Ops:
  7.2 316.3 %copy-start = (bf16[1024,1024]{1,0:T(8,128)(2,1)S(1)}, bf16[1024,1024]{1,0:T(8,128)(2,1)}, u32[]{:S(2)}) copy-start(bf16[1024,1024]{1,0:T(8,128)(2,1)} %param.23) | copy-start | bytes 6291460
  7.2 249.3 %all-gather.4.cloned.1.call-start = ((), (), s32[]{:S(2)}) async-start(), calls=%async_computation.5 | async-start | bytes 5570560 | tf_op jit(solution)/shard_map/all_gather | solution.py:141
  17.8 308.7 %all-gather.6.cloned.1.call-start = ((), (), s32[]{:S(2)}) async-start(), calls=%async_computation.7 | async-start | bytes 5570560 | tf_op jit(solution)/shard_map/all_gather | solution.py:210
  19.9 89.5 %copy-start.23 = (f32[160,8]{1,0:T(8,128)}, f32[160,8]{1,0:T(8,128)S(1)}, u32[]{:S(2)}) copy-start(f32[160,8]{1,0:T(8,128)S(1)} %copy.82) | copy-start | bytes 15364
  27.3 1.8 collective-permute-start
  30.0 19.0 %collective-permute-start.1 = (bf16[2,160,1024]{2,1,0:T(8,128)(2,1)S(1)}, bf16[2,160,1024]{2,1,0:T(8,128)(2,1)}, u32[]{:S(2)}, u32[]{:S(2)}) collective-permute-start(bf16[2,160,1024]{2,1,0:T(8,128)(2,1)S(1)} %pad_maximum_fusion.4), channel_id=1, source_target_pairs={{0,4},{2,6},{4,0},{6,2},{8,12},{10,14},{12,8},{14,10},{16,20},{18,... | collective-permute-start | bytes 1966088 | tf_op jit(solution)/shard_map/ppermute | solution.py:26
  52.4 47.5 %collective-permute-start.2 = (bf16[4,160,1024]{2,1,0:T(8,128)(2,1)}, bf16[4,160,1024]{2,1,0:T(8,128)(2,1)}, u32[]{:S(2)}, u32[]{:S(2)}) collective-permute-start(bf16[4,160,1024]{2,1,0:T(8,128)(2,1)} %pad_maximum_fusion.2), channel_id=1, source_target_pairs={{0,8},{2,10},{4,12},{6,14},{8,0},{10,2},{12,4},{14,6},{16,24},{18,... | collective-permute-start | bytes 3932168 | tf_op jit(solution)/shard_map/ppermute | solution.py:26
  103.9 147.6 %collective-permute-start.3 = (bf16[8,160,1024]{2,1,0:T(8,128)(2,1)}, bf16[8,160,1024]{2,1,0:T(8,128)(2,1)}, u32[]{:S(2)}, u32[]{:S(2)}) collective-permute-start(bf16[8,160,1024]{2,1,0:T(8,128)(2,1)} %pad_maximum_fusion.1), channel_id=1, source_target_pairs={{0,16},{2,18},{4,20},{6,22},{8,24},{10,26},{12,28},{14,30},{16,0},... | collective-permute-start | bytes 7864328 | tf_op jit(solution)/shard_map/ppermute | solution.py:26
  107.5 462.8 %reduce-scatter.8.cloned.1.call-start = ((), (), s32[]{:S(2)}) async-start(), calls=%async_computation.8 | async-start | bytes 11141120 | tf_op jit(solution)/shard_map/reduce_scatter | solution.py:262
  110.9 140.6 %copy-start.8 = (bf16[4,160,1024]{2,1,0:T(8,128)(2,1)S(1)}, bf16[4,160,1024]{2,1,0:T(8,128)(2,1)}, u32[]{:S(2)}) copy-start(bf16[4,160,1024]{2,1,0:T(8,128)(2,1)} %copy-done.7) | copy-start | bytes 3932164
  264.4 59.1 %copy-start.15 = (bf16[1,1,160,1024]{3,2,1,0:T(8,128)(2,1)S(1)}, bf16[1,1,160,1024]{3,2,1,0:T(8,128)(2,1)}, u32[]{:S(2)}) copy-start(bf16[1,1,160,1024]{3,2,1,0:T(8,128)(2,1)} %param.29) | copy-start | bytes 983044
  450.4 191.1 %reduce-scatter.14.cloned.1.call-start = ((), (), s32[]{:S(2)}) async-start(), calls=%async_computation.11 | async-start | bytes 3145728 | tf_op jit(solution)/shard_map/reduce_scatter | solution.py:288
  454.5 237.0 %reduce-scatter.12.cloned.1.call-start = ((), (), s32[]{:S(2)}) async-start(), calls=%async_computation.10 | async-start | bytes 9437184 | tf_op jit(solution)/shard_map/reduce_scatter | solution.py:285
  584.4 17.9 %copy-start.42 = (f32[2048]{0:T(1024)S(1)}, f32[2048]{0:T(1024)}, u32[]{:S(2)}) copy-start(f32[2048]{0:T(1024)} %param.26) | copy-start | bytes 24580
  584.4 125.8 %reduce-scatter.6.cloned.1.call-start = ((), (), s32[]{:S(2)}) async-start(), calls=%async_computation.6 | async-start | bytes 983040 | tf_op jit(solution)/shard_map/reduce_scatter | solution.py:183
  611.5 117.0 %reduce-scatter.10.cloned.1.call-start = ((), (), s32[]{:S(2)}) async-start(), calls=%async_computation.9 | async-start | bytes 983040 | tf_op jit(solution)/shard_map/reduce_scatter | solution.py:201
  630.9 335.8 %all-reduce.9.cloned.1.call-start = ((), (), s32[]{:S(2)}) async-start(), calls=%async_computation.12 | async-start | bytes 25165824 | tf_op jit(solution)/shard_map/psum | solution.py:305
  691.4 18.8 %copy-start.10 = (bf16[1,1,160,1024]{3,2,1,0:T(8,128)(2,1)S(1)}, bf16[1,1,160,1024]{3,2,1,0:T(8,128)(2,1)}, u32[]{:S(2)}) copy-start(bf16[1,1,160,1024]{3,2,1,0:T(8,128)(2,1)} %param.17) | copy-start | bytes 983044
  691.4 18.8 %copy-start.31 = (f32[1024]{0:T(1024)S(1)}, f32[1024]{0:T(1024)}, u32[]{:S(2)}) copy-start(f32[1024]{0:T(1024)} %param.28) | copy-start | bytes 12292
  691.4 18.8 %copy-start.32 = (f32[1024]{0:T(1024)S(1)}, f32[1024]{0:T(1024)}, u32[]{:S(2)}) copy-start(f32[1024]{0:T(1024)} %param.24) | copy-start | bytes 12292
  691.5 37.1 %copy-start.34 = (f32[160]{0:T(256)S(1)}, f32[160]{0:T(256)}, u32[]{:S(2)}) copy-start(f32[160]{0:T(256)} %copy-done.33) | copy-start | bytes 1924
  691.5 37.1 %copy-start.35 = (f32[1024]{0:T(1024)S(1)}, f32[1024]{0:T(1024)}, u32[]{:S(2)}) copy-start(f32[1024]{0:T(1024)} %param.19) | copy-start | bytes 12292
  691.5 37.1 %copy-start.37 = (f32[160]{0:T(256)S(1)}, f32[160]{0:T(256)}, u32[]{:S(2)}) copy-start(f32[160]{0:T(256)} %copy-done.36) | copy-start | bytes 1924
  806.3 176.9 %copy-start.38 = (f32[512]{0:T(512)}, f32[512]{0:T(512)S(1)}, u32[]{:S(2)}) copy-start(f32[512]{0:T(512)S(1)} %convert_element_type.187) | copy-start | bytes 6148
  (48 other events, 242.8 us)
Sparse Core Ops, SparseCore 0:
  17.9 66.8 all-gather.3
  107.6 114.6 all-gather.5
  450.6 119.6 reduce-scatter.7
  573.0 38.5 reduce-scatter.13
  614.3 77.1 reduce-scatter.11
  694.1 16.0 reduce-scatter.5
  712.5 16.0 reduce-scatter.9
  733.7 232.9 all-reduce.8
